TPU v7x, 32 devices: a whole 2x2x4 slice. The times are simulated.
32 devices in a mesh: expert: 8 (over z, x), dp: 4 (over y, core).
Axes of the slice: x: 2, y: 2, z: 4, core: 2. Of those that a mesh axis runs over, the one named last changes fastest.
Arguments:
- grad_output: bfloat16 [4096, 2048], P(('expert', 'dp')), may hold values from -1.5 to 1.5
- logits: float32 [4096, 8], P(('expert', 'dp')), may hold values from -6 to 6
- chosen: int32 [4096, 8], P(('expert', 'dp')), may hold values from 0 to 31, as said below
- slots: int32 [4096, 8], P(('expert', 'dp')), may hold values from 0 to 40, as said below
- other_scores: float32 [4096, 8], P(('expert', 'dp')), may hold values from -48 to 48
- hidden: bfloat16 [8, 4, 8, 40, 768], P('expert', 'dp'), may hold values from -6 to 6
- down_weight: bfloat16 [8, 768, 2048], P('expert', 'dp'), may hold values from -0.21875 to 0.21875
Outputs:
- grad_hidden: bfloat16 [8, 4, 8, 40, 768], P('expert', 'dp')
- grad_down: float32 [8, 768, 2048], P('expert', 'dp')
- grad_logits: float32 [4096, 8], P(('expert', 'dp'))
Inputs may be any that keep to these rules, and one draw needn't show every extreme that they name: `chosen`: each row names 8 different experts. 40 marks a choice with no slot: its expert is 8 or above, or it comes after 40 earlier choices of the same expert among the rows of one device in row-major order. The live choices of one expert on one device hold slots 0, 1, 2, ... in that order. Some expert fills all 40 slots on some device.
All inputs are finite; a program needn't handle non-finite values.
Results may differ from a plain program's by a relative error of at most 0.023.
Values may be sent and summed in bfloat16 or wider, within the bound.
A program may use at most 64 MiB of HBM per device.

v0:
```python
import functools

import jax
import jax.numpy as jnp
from jax import lax
from jax.experimental import pallas as pl
from jax.experimental.pallas import tpu as pltpu
from jax.sharding import PartitionSpec as P

MESH = pl.DeviceIdType.MESH
PIECES = 8


def kernel(
    window, shards, capacity, pieces,
    token_hbm, logits_hbm, chosen_hbm, slots_hbm, other_hbm, hidden_hbm, weight_ref,
    gradh_ref, down_ref, logit_ref,
    token_ref, logits_ref, chosen_ref, slots_ref, other_ref, hidden_ref,
    rsend, rrecv, msend, mrecv, wfull, padded, hturn, upward, own, csend, crecv, ysend, yrecv,
    tsend, trecv, gates,
    rs, rr, ms, mr, ws, wr, fs, fr, cs, cr, ys, yr, ts, tr, ls, lw,
):
    me = lax.axis_index("expert")
    place = lax.axis_index("dp")
    chip, core = place // 2, place % 2
    chips = shards // 2
    mate = (me, chip * 2 + 1 - core)
    tokens, width = token_ref.shape
    piece = width // pieces
    rows = rsend.shape[2]
    slots_all = window * rows
    shard_rows, hidden_units = weight_ref.shape[0], hidden_ref.shape[2]

    near = [lax.rem(me + step, window) for step in range(window)]

    def other(step):
        return near[step]

    def settle(buffer, sem):
        whole = buffer.at[pl.ds(0, window - 1)]
        pltpu.make_async_copy(whole, whole, sem).wait()

    def chip_at(step):
        return lax.rem(chip + step, chips)

    def across(step):
        return (me, chip_at(step) * 2 + core)

    loads = [
        pltpu.make_async_copy(src, dst, ls.at[i])
        for i, (src, dst) in enumerate((
            (chosen_hbm, chosen_ref), (slots_hbm, slots_ref), (token_hbm, token_ref),
            (logits_hbm, logits_ref), (other_hbm, other_ref), (hidden_hbm, hidden_ref),
        ))
    ]
    for load in loads:
        load.start()
    keeps = [
        pltpu.make_async_copy(
            weight_ref.at[:, pl.ds(c * piece, piece)], wfull.at[c, place], lw.at[c]
        )
        for c in range(pieces)
    ]

    def weight_copy(c, target, step, slot):
        lanes = pl.ds(pl.multiple_of(c * piece, piece), piece)
        return pltpu.make_async_remote_copy(
            src_ref=weight_ref.at[:, lanes], dst_ref=wfull.at[c, slot],
            send_sem=ws.at[c, step], recv_sem=wr.at[c, step],
            device_id=target, device_id_type=MESH,
        )

    barrier = pltpu.get_barrier_semaphore()
    for step in range(1, window):
        pl.semaphore_signal(barrier, inc=1, device_id=(other(step), place), device_id_type=MESH)
    for step in range(1, chips):
        pl.semaphore_signal(barrier, inc=1, device_id=across(step), device_id_type=MESH)
    pl.semaphore_signal(barrier, inc=1, device_id=mate, device_id_type=MESH)

    k = logit_ref.shape[0]
    for load in loads[:5]:
        load.wait()
    raised = jnp.exp(logits_ref[...])
    gating = raised / jnp.sum(raised, axis=0, keepdims=True)
    sent_gate = gating.astype(jnp.bfloat16).astype(jnp.float32)
    chosen = chosen_ref[...]
    slots = slots_ref[...]
    outside = jnp.where(chosen >= window, other_ref[...], 0.0)
    live = slots < capacity
    for w in range(window):
        here = live & (chosen == w)
        pos = jnp.sum(jnp.where(here, slots.astype(jnp.float32) + 1.0, 0.0), axis=0, keepdims=True) - 1.0
        gate = jnp.sum(jnp.where(here, sent_gate, 0.0), axis=0, keepdims=True)
        line = lax.broadcasted_iota(jnp.int32, (8, tokens), 0)
        msend[w] = jnp.where(line == 0, pos, gate)

    slot_id = lax.broadcasted_iota(jnp.int32, (rows, tokens), 0).astype(jnp.float32)

    def spread(ref, w):
        return slot_id == ref[w, 0:1, :]

    dispatch = jnp.concatenate(
        [spread(msend, w).astype(jnp.float32) for w in range(window)], axis=0
    ).astype(jnp.bfloat16)

    def fill(c):
        lanes = pl.ds(pl.multiple_of(c * piece, piece), piece)
        placed = jnp.dot(dispatch, token_ref[:, lanes], preferred_element_type=jnp.float32)
        rsend[c] = placed.astype(jnp.bfloat16).reshape(window, rows, piece)

    def row_copy(c, dest, source):
        return pltpu.make_async_remote_copy(
            src_ref=rsend.at[c, dest, pl.ds(0, capacity)],
            dst_ref=rrecv.at[c, source, pl.ds(0, capacity)],
            send_sem=rs, recv_sem=rr.at[c],
            device_id=(dest, place), device_id_type=MESH,
        )

    def meta_copy(dest, source):
        return pltpu.make_async_remote_copy(
            src_ref=msend.at[dest], dst_ref=mrecv.at[source],
            send_sem=ms, recv_sem=mr,
            device_id=(dest, place), device_id_type=MESH,
        )

    def score_copy(dest, source):
        return pltpu.make_async_remote_copy(
            src_ref=tsend.at[dest], dst_ref=trecv.at[source],
            send_sem=ts, recv_sem=tr,
            device_id=(dest, place), device_id_type=MESH,
        )

    def pass_copy(c, step, slot):
        return pltpu.make_async_remote_copy(
            src_ref=wfull.at[c, slot], dst_ref=wfull.at[c, slot],
            send_sem=fs.at[c, step], recv_sem=fr.at[c, step],
            device_id=mate, device_id_type=MESH,
        )

    def core_copy(c):
        return pltpu.make_async_remote_copy(
            src_ref=csend.at[c], dst_ref=crecv.at[c],
            send_sem=cs.at[c], recv_sem=cr.at[c],
            device_id=mate, device_id_type=MESH,
        )

    def sum_copy(c, step):
        return pltpu.make_async_remote_copy(
            src_ref=ysend.at[c, step], dst_ref=yrecv.at[c, step],
            send_sem=ys.at[c, step], recv_sem=yr.at[c, step],
            device_id=across(step), device_id_type=MESH,
        )

    fill(0)
    pl.semaphore_wait(barrier, window - 1 + chips)

    def launch_weights(c, carry):
        for step in range(1, chips):
            weight_copy(c, across(step), step, place).start()
        weight_copy(c, mate, 0, place).start()
        return carry

    lax.fori_loop(0, pieces, launch_weights, 0)

    for step in range(1, window):
        meta_copy(other(step), me).start()

    def launch(c, carry):
        for step in range(1, window):
            row_copy(c, other(step), me).start()

        @pl.when(c + 1 < pieces)
        def _():
            fill(c + 1)

        return carry

    lax.fori_loop(0, pieces, launch, 0)

    mrecv[me] = msend[me]
    for c in range(pieces):
        rrecv[c, me, 0:capacity] = rsend[c, me, 0:capacity]
        if rows > capacity:
            rrecv[c, :, capacity:rows] = jnp.zeros((window, rows - capacity, piece), jnp.bfloat16)
        keeps[c].start()
    loads[5].wait()
    padded[:, 0:capacity] = hidden_ref[...]
    if rows > capacity:
        padded[:, capacity:rows] = jnp.zeros((window, rows - capacity, hidden_units), jnp.bfloat16)
    flat = padded[...].reshape(slots_all, hidden_units)
    hturn[...] = flat.T.reshape(shards, shard_rows, slots_all)
    upward[...] = jnp.zeros_like(upward)
    for keep in keeps:
        keep.wait()

    settle(mrecv, mr)
    for s in range(window):
        gates[s] = jnp.sum(
            jnp.where(spread(mrecv, s), mrecv[s, 1:2, :], 0.0), axis=1, keepdims=True
        )

    def combine(c):
        lanes = pl.ds(pl.multiple_of(c * piece, piece), piece)
        core_copy(c).wait_recv()
        for step in range(1, chips):
            to = chip_at(step)
            ysend[c, step] = (own[c, to] + crecv[c, to].astype(jnp.float32)).astype(jnp.bfloat16)
            sum_copy(c, step).start()
        down_ref[:, lanes] = own[c, chip] + crecv[c, chip].astype(jnp.float32)

    def finish(c, carry):
        for step in range(1, chips):
            came = lax.rem(chip + chips - step, chips) * 2 + core
            weight_copy(c, across(step), step, came).wait_recv()
            pass_copy(c, step, came).start()
        came_rows = rrecv.at[c, pl.ds(0, window - 1), pl.ds(0, capacity)]
        pltpu.make_async_copy(came_rows, came_rows, rr.at[c]).wait()
        got = rrecv[c].reshape(slots_all, piece)
        scaled = (gates[...].reshape(slots_all, 1) * got.astype(jnp.float32)).astype(jnp.bfloat16)
        for h in range(chips):
            csend[c, h] = jnp.dot(
                hturn[2 * h + 1 - core], scaled, preferred_element_type=jnp.float32
            ).astype(jnp.bfloat16)
        core_copy(c).start()
        for h in range(chips):
            own[c, h] = jnp.dot(hturn[2 * h + core], scaled, preferred_element_type=jnp.float32)
        weight_copy(c, mate, 0, chip * 2 + 1 - core).wait_recv()
        for step in range(1, chips):
            came = lax.rem(chip + chips - step, chips) * 2 + 1 - core
            pass_copy(c, step, came).wait_recv()
        weights = wfull[c].reshape(hidden_units, piece)
        upward[...] += lax.dot_general(
            got, weights, (((1,), (1,)), ((), ())), preferred_element_type=jnp.float32
        )

        @pl.when(c > 0)
        def _():
            combine(c - 1)

        return carry

    lax.fori_loop(0, pieces, finish, 0)
    combine(pieces - 1)

    for s in range(window):
        up = upward[s * rows : (s + 1) * rows]
        score = jnp.sum(padded[s].astype(jnp.float32) * up, axis=1, keepdims=True)
        back = jnp.sum(jnp.where(spread(mrecv, s), score, 0.0), axis=0, keepdims=True)
        tsend[s] = jnp.broadcast_to(back, (8, tokens))
    for step in range(1, window):
        score_copy(other(step), me).start()
    trecv[me] = tsend[me]
    for s in range(window):
        up = upward[s * rows : s * rows + capacity]
        gradh_ref[s] = (gates[s, 0:capacity] * up).astype(jnp.bfloat16)

    def collect(c, carry):
        lanes = pl.ds(pl.multiple_of(c * piece, piece), piece)
        for step in range(1, chips):
            sum_copy(c, step).wait_recv()
            down_ref[:, lanes] += yrecv[c, step].astype(jnp.float32)
        return carry

    def drain(c, carry):
        for step in range(1, chips):
            weight_copy(c, across(step), step, place).wait_send()
            pass_copy(c, step, lax.rem(chip + chips - step, chips) * 2 + core).wait_send()
        weight_copy(c, mate, 0, place).wait_send()
        core_copy(c).wait_send()
        return carry

    lax.fori_loop(0, pieces, drain, 0)
    sent_rows = rsend.at[:, pl.ds(0, window - 1), pl.ds(0, capacity)]
    pltpu.make_async_copy(sent_rows, sent_rows, rs).wait()
    settle(msend, ms)
    lax.fori_loop(0, pieces - 1, collect, 0)

    settle(trecv, tr)
    token_scores = jnp.zeros((k, tokens), jnp.float32)
    for w in range(window):
        token_scores = jnp.where(chosen == w, trecv[w], token_scores)
    scores_all = jnp.where(live, token_scores, outside)
    mean_score = jnp.sum(gating * scores_all, axis=0, keepdims=True)
    logit_ref[...] = gating * (scores_all - mean_score)
    settle(tsend, ts)

    collect(pieces - 1, 0)
    for c in range(pieces):
        for step in range(1, chips):
            sum_copy(c, step).wait_send()


def write_out(a, b, c, a_out, b_out, c_out, sems):
    copies = [
        pltpu.make_async_copy(src, dst, sems.at[i])
        for i, (src, dst) in enumerate(((b, b_out), (a, a_out), (c, c_out)))
    ]
    for copy in copies:
        copy.start()
    for copy in copies:
        copy.wait()


def fused(grad_output, logits, chosen, slots, other_scores, hidden, down_weight):
    window = lax.axis_size("expert")
    shards = lax.axis_size("dp")
    capacity, hidden_units = hidden.shape[3], hidden.shape[4]
    tokens, width = grad_output.shape
    k = logits.shape[1]
    shard_rows = down_weight.shape[1]
    rows = -(-capacity // 16) * 16
    chips = shards // 2
    piece = width // PIECES
    vmem = pl.BlockSpec(memory_space=pltpu.VMEM)
    hbm = pl.BlockSpec(memory_space=pltpu.HBM)
    bf, f32, dma = jnp.bfloat16, jnp.float32, pltpu.SemaphoreType.DMA
    slots_all = window * rows
    gradh, down, turned = pl.pallas_call(
        functools.partial(kernel, window, shards, capacity, PIECES),
        out_shape=(
            jax.ShapeDtypeStruct((window, capacity, hidden_units), bf),
            jax.ShapeDtypeStruct((shard_rows, width), f32),
            jax.ShapeDtypeStruct((k, tokens), f32),
        ),
        in_specs=[hbm] * 7,
        out_specs=(vmem,) * 3,
        scratch_shapes=[
            pltpu.VMEM((tokens, width), bf),
            pltpu.VMEM((k, tokens), f32),
            pltpu.VMEM((k, tokens), jnp.int32),
            pltpu.VMEM((k, tokens), jnp.int32),
            pltpu.VMEM((k, tokens), f32),
            pltpu.VMEM((window, capacity, hidden_units), bf),
            pltpu.VMEM((PIECES, window, rows, piece), bf),
            pltpu.VMEM((PIECES, window, rows, piece), bf),
            pltpu.VMEM((window, 8, tokens), f32),
            pltpu.VMEM((window, 8, tokens), f32),
            pltpu.VMEM((PIECES, shards, shard_rows, piece), bf),
            pltpu.VMEM((window, rows, hidden_units), bf),
            pltpu.VMEM((shards, shard_rows, slots_all), bf),
            pltpu.VMEM((slots_all, hidden_units), f32),
            pltpu.VMEM((PIECES, chips, shard_rows, piece), f32),
            pltpu.VMEM((PIECES, chips, shard_rows, piece), bf),
            pltpu.VMEM((PIECES, chips, shard_rows, piece), bf),
            pltpu.VMEM((PIECES, chips, shard_rows, piece), bf),
            pltpu.VMEM((PIECES, chips, shard_rows, piece), bf),
            pltpu.VMEM((window, 8, tokens), f32),
            pltpu.VMEM((window, 8, tokens), f32),
            pltpu.VMEM((window, rows, 1), f32),
            dma, dma((PIECES,)),
            dma, dma,
            dma((PIECES, chips)), dma((PIECES, chips)),
            dma((PIECES, chips)), dma((PIECES, chips)),
            dma((PIECES,)), dma((PIECES,)),
            dma((PIECES, chips)), dma((PIECES, chips)),
            dma, dma,
            dma((6,)), dma((PIECES,)),
        ],
        compiler_params=pltpu.CompilerParams(
            collective_id=0, has_side_effects=True, vmem_limit_bytes=48 * 1024 * 1024
        ),
    )(*(pltpu.with_memory_space_constraint(a, pltpu.HBM) for a in (
        grad_output, logits.T, chosen.T, slots.T, other_scores.T,
        hidden.reshape(window, capacity, hidden_units), down_weight.reshape(shard_rows, width),
    )))
    gradh, down, turned = (
        pltpu.with_memory_space_constraint(a, pltpu.VMEM) for a in (gradh, down, turned)
    )
    gradh, down, turned = pl.pallas_call(
        write_out,
        out_shape=tuple(jax.ShapeDtypeStruct(a.shape, a.dtype) for a in (gradh, down, turned)),
        in_specs=[vmem] * 3,
        out_specs=(hbm,) * 3,
        scratch_shapes=[dma((3,))],
        compiler_params=pltpu.CompilerParams(vmem_limit_bytes=8 * 1024 * 1024),
    )(gradh, down, turned)
    return (gradh.reshape(hidden.shape), down.reshape(1, shard_rows, width), turned.T)


def plain(grad_output, logits, chosen, slots, other_scores, hidden, down_weight):
    window = lax.axis_size("expert")
    capacity = hidden.shape[3]
    hidden_units = hidden.shape[4]
    model_width = grad_output.shape[1]
    shard_rows = down_weight.shape[1]
    raised = jnp.exp(logits)
    gating = raised / jnp.sum(raised, axis=1, keepdims=True)
    gate_sent = gating.astype(jnp.bfloat16)
    live_slot = slots < capacity
    target = jnp.where(live_slot, chosen * capacity + slots, window * capacity)
    columns = jnp.arange(window * capacity, dtype=jnp.int32)
    placing = (target[:, :, None] == columns[None, None, :]).astype(jnp.bfloat16)
    dispatch = jnp.sum(placing, axis=1)
    send_rows = jnp.einsum(
        "tr,td->rd", dispatch, grad_output, preferred_element_type=jnp.float32
    ).astype(jnp.bfloat16)
    send_gate = jnp.einsum(
        "tkr,tk->r", placing, gate_sent, preferred_element_type=jnp.float32
    ).astype(jnp.bfloat16)
    placing_float = placing.astype(jnp.float32)
    send_rows = send_rows.reshape(window, capacity, model_width)
    send_gate = send_gate.reshape(window, capacity)
    recv_rows, recv_gate = (
        lax.all_to_all(send_rows, "expert", split_axis=0, concat_axis=0, tiled=True),
        lax.all_to_all(send_gate, "expert", split_axis=0, concat_axis=0, tiled=True),
    )
    slot_rows = recv_rows.reshape(-1, model_width)
    slot_gate = recv_gate.reshape(-1).astype(jnp.float32)
    local_hidden = hidden.reshape(-1, hidden_units)
    scaled = (slot_gate[:, None] * slot_rows.astype(jnp.float32)).astype(jnp.bfloat16)
    weights = down_weight.reshape(shard_rows, model_width)
    product = lax.dot_general(
        slot_rows,
        lax.all_gather(weights, "dp", axis=0, tiled=True),
        (((1,), (1,)), ((), ())),
        preferred_element_type=jnp.float32,
    )
    grad_rows = lax.psum_scatter(
        lax.dot_general(
            local_hidden, scaled, (((0,), (0,)), ((), ())), preferred_element_type=jnp.float32
        ).astype(jnp.bfloat16),
        "dp",
        scatter_dimension=0,
        tiled=True,
    ).astype(jnp.float32)
    slot_scores = jnp.sum(local_hidden.astype(jnp.float32) * product, axis=1)
    grad_hidden = (slot_gate[:, None] * product).astype(jnp.bfloat16).reshape(hidden.shape)
    returned = lax.all_to_all(
        slot_scores.reshape(window, capacity), "expert", split_axis=0, concat_axis=0, tiled=True
    )
    token_scores = jnp.einsum(
        "tkr,r->tk", placing_float, returned.reshape(-1), precision=lax.Precision.HIGHEST
    )
    outside = jnp.where(chosen >= window, other_scores, jnp.float32(0.0))
    scores_all = jnp.where(live_slot, token_scores, outside)
    mean_score = jnp.sum(gating * scores_all, axis=1, keepdims=True)
    grad_logits = gating * (scores_all - mean_score)
    return (grad_hidden, grad_rows.reshape(1, shard_rows, model_width), grad_logits)


def body(grad_output, logits, chosen, slots, other_scores, hidden, down_weight):
    args = (grad_output, logits, chosen, slots, other_scores, hidden, down_weight)
    fits = (
        lax.axis_size("dp") % 2 == 0
        and hidden.shape[3] % 8 == 0
        and down_weight.shape[1] % 16 == 0
        and hidden.shape[4] % 128 == 0
        and grad_output.shape[0] == 128
        and grad_output.shape[1] % (PIECES * 128) == 0
        and logits.shape[1] == 8
    )
    return fused(*args) if fits else plain(*args)


def solution(mesh):
    placed = (
        P(("expert", "dp"), None),
        P(("expert", "dp"), None),
        P(("expert", "dp"), None),
        P(("expert", "dp"), None),
        P(("expert", "dp"), None),
        P("expert", "dp", None, None, None),
        P("expert", "dp", None),
    )
    return jax.shard_map(
        body,
        mesh=mesh,
        in_specs=placed,
        out_specs=(
            P("expert", "dp", None, None, None),
            P("expert", "dp", None),
            P(("expert", "dp"), None),
        ),
        check_vma=False,
    )
```

profile of v0, /device:TPU:0, one launch (start us, length us, event | category | flops | bytes accessed | tf_op | source)
XLA Modules:
  0.0 47.2 jit_solution(12415989593689603870)
XLA Ops:
  0.6 45.3 %shard_map.94 = (bf16[8,40,768]{2,1,0:T(8,128)(2,1)S(1)}, f32[192,2048]{1,0:T(8,128)S(1)}, f32[8,128]{1,0:T(8,128)S(1)}) custom-call(bf16[128,2048]{1,0:T(8,128)(2,1)} %token_hbm.1, f32[8,128]{1,0:T(8,128)} %bitcast.11, s32[8,128]{1,0:T(8,128)} %bitcast.12, s32[8,128]{1,0:T(8,128)} %bitcast.13, f32[8,128]{1,0:T(8,128)} %bitcast.14, ...), custom_call_target="tpu_custom_call" | custom-call | tf_op jit(solution)/shard_map/pallas_call | solution.py:318
  45.9 1.3 %shard_map.95 = (bf16[8,40,768]{2,1,0:T(8,128)(2,1)}, f32[192,2048]{1,0:T(8,128)}, f32[8,128]{1,0:T(8,128)}) custom-call(bf16[8,40,768]{2,1,0:T(8,128)(2,1)S(1)} %get-tuple-element.9.a, f32[192,2048]{1,0:T(8,128)S(1)} %get-tuple-element.10.b, f32[8,128]{1,0:T(8,128)S(1)} %get-tuple-element.11.c), custom_call_target="tpu_custom_call" | custom-call | tf_op jit(solution)/shard_map/pallas_call | solution.py:369
where the time goes:
time: 47.4 us; the launch traced here: 47.2 us
  Pallas kernels  46.6 us (98%)
  between operations  0.64 us (1%)
    pallas_call x1, Pallas kernels, fused(): pl.pallas_call(functools.partial(kernel, window, shards, capacity, PIECES...  45.3 us
    pallas_call x1, Pallas kernels, fused(): pl.pallas_call(write_out, out_shape=tuple((jax.ShapeDtypeStruct(a.shape,...  1.33 us

commit v1 on v0

--- a/solution.py
+++ b/solution.py
@@ -9,16 +9,17 @@
 
 MESH = pl.DeviceIdType.MESH
 PIECES = 8
+AHEAD = 3
 
 
 def kernel(
-    window, shards, capacity, pieces,
+    window, shards, capacity, pieces, ahead,
     token_hbm, logits_hbm, chosen_hbm, slots_hbm, other_hbm, hidden_hbm, weight_ref,
     gradh_ref, down_ref, logit_ref,
     token_ref, logits_ref, chosen_ref, slots_ref, other_ref, hidden_ref,
     rsend, rrecv, msend, mrecv, wfull, padded, hturn, upward, own, csend, crecv, ysend, yrecv,
     tsend, trecv, gates,
-    rs, rr, ms, mr, ws, wr, fs, fr, cs, cr, ys, yr, ts, tr, ls, lw,
+    rs, rr, ms, mr, ws, wr, dr, fs, cs, cr, ys, yr, ts, tr, ls, lw,
 ):
     me = lax.axis_index("expert")
     place = lax.axis_index("dp")
@@ -31,7 +32,17 @@
     slots_all = window * rows
     shard_rows, hidden_units = weight_ref.shape[0], hidden_ref.shape[2]
 
-    near = [lax.rem(me + step, window) for step in range(window)]
+    def flipped(mask):
+        where = me
+        for bit in range(window.bit_length() - 1):
+            if mask >> bit & 1:
+                where = where + (1 << bit) * (1 - 2 * (me // (1 << bit) % 2))
+        return where
+
+    if window & (window - 1):
+        near = [lax.rem(me + step, window) for step in range(window)]
+    else:
+        near = [flipped(mask) for mask in (0, *range(window - 1, 0, -1))]
 
     def other(step):
         return near[step]
@@ -57,16 +68,16 @@
         load.start()
     keeps = [
         pltpu.make_async_copy(
-            weight_ref.at[:, pl.ds(c * piece, piece)], wfull.at[c, place], lw.at[c]
+            weight_ref.at[:, pl.ds(c * piece, piece)], wfull.at[c, place], lw
         )
         for c in range(pieces)
     ]
 
-    def weight_copy(c, target, step, slot):
+    def weight_copy(c, target, sem):
         lanes = pl.ds(pl.multiple_of(c * piece, piece), piece)
         return pltpu.make_async_remote_copy(
-            src_ref=weight_ref.at[:, lanes], dst_ref=wfull.at[c, slot],
-            send_sem=ws.at[c, step], recv_sem=wr.at[c, step],
+            src_ref=weight_ref.at[:, lanes], dst_ref=wfull.at[c, place],
+            send_sem=ws, recv_sem=sem,
             device_id=target, device_id_type=MESH,
         )
 
@@ -130,24 +141,24 @@
             device_id=(dest, place), device_id_type=MESH,
         )
 
-    def pass_copy(c, step, slot):
+    def pass_copy(c, slot):
         return pltpu.make_async_remote_copy(
             src_ref=wfull.at[c, slot], dst_ref=wfull.at[c, slot],
-            send_sem=fs.at[c, step], recv_sem=fr.at[c, step],
+            send_sem=fs, recv_sem=dr.at[c],
             device_id=mate, device_id_type=MESH,
         )
 
     def core_copy(c):
         return pltpu.make_async_remote_copy(
             src_ref=csend.at[c], dst_ref=crecv.at[c],
-            send_sem=cs.at[c], recv_sem=cr.at[c],
+            send_sem=cs, recv_sem=cr.at[c],
             device_id=mate, device_id_type=MESH,
         )
 
     def sum_copy(c, step):
         return pltpu.make_async_remote_copy(
-            src_ref=ysend.at[c, step], dst_ref=yrecv.at[c, step],
-            send_sem=ys.at[c, step], recv_sem=yr.at[c, step],
+            src_ref=ysend.at[c, step - 1], dst_ref=yrecv.at[c, step - 1],
+            send_sem=ys, recv_sem=yr.at[c],
             device_id=across(step), device_id_type=MESH,
         )
 
@@ -156,8 +167,8 @@
 
     def launch_weights(c, carry):
         for step in range(1, chips):
-            weight_copy(c, across(step), step, place).start()
-        weight_copy(c, mate, 0, place).start()
+            weight_copy(c, across(step), wr.at[c, step - 1]).start()
+        weight_copy(c, mate, dr.at[c]).start()
         return carry
 
     lax.fori_loop(0, pieces, launch_weights, 0)
@@ -165,9 +176,14 @@
     for step in range(1, window):
         meta_copy(other(step), me).start()
 
-    def launch(c, carry):
+    def send_rows(c):
         for step in range(1, window):
             row_copy(c, other(step), me).start()
+
+    def launch(c, carry):
+        @pl.when(c < ahead)
+        def _():
+            send_rows(c)
 
         @pl.when(c + 1 < pieces)
         def _():
@@ -201,20 +217,31 @@
 
     def combine(c):
         lanes = pl.ds(pl.multiple_of(c * piece, piece), piece)
-        core_copy(c).wait_recv()
+        with jax.named_scope("w_core"):
+            core_copy(c).wait_recv()
         for step in range(1, chips):
             to = chip_at(step)
-            ysend[c, step] = (own[c, to] + crecv[c, to].astype(jnp.float32)).astype(jnp.bfloat16)
+            ysend[c, step - 1] = (own[c, to] + crecv[c, to].astype(jnp.float32)).astype(jnp.bfloat16)
             sum_copy(c, step).start()
         down_ref[:, lanes] = own[c, chip] + crecv[c, chip].astype(jnp.float32)
 
     def finish(c, carry):
+        @pl.when(c > 0)
+        def _():
+            combine(c - 1)
+
         for step in range(1, chips):
             came = lax.rem(chip + chips - step, chips) * 2 + core
-            weight_copy(c, across(step), step, came).wait_recv()
-            pass_copy(c, step, came).start()
+            weight_copy(c, mate, wr.at[c, step - 1]).wait_recv()
+            pass_copy(c, came).start()
         came_rows = rrecv.at[c, pl.ds(0, window - 1), pl.ds(0, capacity)]
-        pltpu.make_async_copy(came_rows, came_rows, rr.at[c]).wait()
+        with jax.named_scope("w_rows"):
+            pltpu.make_async_copy(came_rows, came_rows, rr.at[c]).wait()
+
+        @pl.when(c + ahead < pieces)
+        def _():
+            send_rows(c + ahead)
+
         got = rrecv[c].reshape(slots_all, piece)
         scaled = (gates[...].reshape(slots_all, 1) * got.astype(jnp.float32)).astype(jnp.bfloat16)
         for h in range(chips):
@@ -224,19 +251,13 @@
         core_copy(c).start()
         for h in range(chips):
             own[c, h] = jnp.dot(hturn[2 * h + core], scaled, preferred_element_type=jnp.float32)
-        weight_copy(c, mate, 0, chip * 2 + 1 - core).wait_recv()
-        for step in range(1, chips):
-            came = lax.rem(chip + chips - step, chips) * 2 + 1 - core
-            pass_copy(c, step, came).wait_recv()
+        with jax.named_scope("w_mate"):
+            from_mate = wfull.at[c, pl.ds(0, chips)]
+            pltpu.make_async_copy(from_mate, from_mate, dr.at[c]).wait()
         weights = wfull[c].reshape(hidden_units, piece)
         upward[...] += lax.dot_general(
             got, weights, (((1,), (1,)), ((), ())), preferred_element_type=jnp.float32
         )
-
-        @pl.when(c > 0)
-        def _():
-            combine(c - 1)
-
         return carry
 
     lax.fori_loop(0, pieces, finish, 0)
@@ -256,22 +277,20 @@
 
     def collect(c, carry):
         lanes = pl.ds(pl.multiple_of(c * piece, piece), piece)
+        with jax.named_scope("w_sum"):
+            came = yrecv.at[c]
+            pltpu.make_async_copy(came, came, yr.at[c]).wait()
         for step in range(1, chips):
-            sum_copy(c, step).wait_recv()
-            down_ref[:, lanes] += yrecv[c, step].astype(jnp.float32)
+            down_ref[:, lanes] += yrecv[c, step - 1].astype(jnp.float32)
         return carry
 
-    def drain(c, carry):
-        for step in range(1, chips):
-            weight_copy(c, across(step), step, place).wait_send()
-            pass_copy(c, step, lax.rem(chip + chips - step, chips) * 2 + core).wait_send()
-        weight_copy(c, mate, 0, place).wait_send()
-        core_copy(c).wait_send()
-        return carry
-
-    lax.fori_loop(0, pieces, drain, 0)
-    sent_rows = rsend.at[:, pl.ds(0, window - 1), pl.ds(0, capacity)]
-    pltpu.make_async_copy(sent_rows, sent_rows, rs).wait()
+    def sent(whole, sem):
+        pltpu.make_async_copy(whole, whole, sem).wait()
+
+    sent(wfull.at[:, pl.ds(0, chips)], ws)
+    sent(wfull.at[:, pl.ds(0, chips - 1)], fs)
+    sent(csend, cs)
+    sent(rsend.at[:, pl.ds(0, window - 1), pl.ds(0, capacity)], rs)
     settle(msend, ms)
     lax.fori_loop(0, pieces - 1, collect, 0)
 
@@ -285,9 +304,7 @@
     settle(tsend, ts)
 
     collect(pieces - 1, 0)
-    for c in range(pieces):
-        for step in range(1, chips):
-            sum_copy(c, step).wait_send()
+    sent(ysend, ys)
 
 
 def write_out(a, b, c, a_out, b_out, c_out, sems):
@@ -316,7 +333,7 @@
     bf, f32, dma = jnp.bfloat16, jnp.float32, pltpu.SemaphoreType.DMA
     slots_all = window * rows
     gradh, down, turned = pl.pallas_call(
-        functools.partial(kernel, window, shards, capacity, PIECES),
+        functools.partial(kernel, window, shards, capacity, PIECES, min(AHEAD, PIECES)),
         out_shape=(
             jax.ShapeDtypeStruct((window, capacity, hidden_units), bf),
             jax.ShapeDtypeStruct((shard_rows, width), f32),
@@ -342,19 +359,19 @@
             pltpu.VMEM((PIECES, chips, shard_rows, piece), f32),
             pltpu.VMEM((PIECES, chips, shard_rows, piece), bf),
             pltpu.VMEM((PIECES, chips, shard_rows, piece), bf),
-            pltpu.VMEM((PIECES, chips, shard_rows, piece), bf),
-            pltpu.VMEM((PIECES, chips, shard_rows, piece), bf),
+            pltpu.VMEM((PIECES, chips - 1, shard_rows, piece), bf),
+            pltpu.VMEM((PIECES, chips - 1, shard_rows, piece), bf),
             pltpu.VMEM((window, 8, tokens), f32),
             pltpu.VMEM((window, 8, tokens), f32),
             pltpu.VMEM((window, rows, 1), f32),
             dma, dma((PIECES,)),
             dma, dma,
-            dma((PIECES, chips)), dma((PIECES, chips)),
-            dma((PIECES, chips)), dma((PIECES, chips)),
-            dma((PIECES,)), dma((PIECES,)),
-            dma((PIECES, chips)), dma((PIECES, chips)),
+            dma, dma((PIECES, chips - 1)), dma((PIECES,)),
+            dma,
+            dma, dma((PIECES,)),
+            dma, dma((PIECES,)),
             dma, dma,
-            dma((6,)), dma((PIECES,)),
+            dma((6,)), dma,
         ],
         compiler_params=pltpu.CompilerParams(
             collective_id=0, has_side_effects=True, vmem_limit_bytes=48 * 1024 * 1024
@@ -442,6 +459,7 @@
     args = (grad_output, logits, chosen, slots, other_scores, hidden, down_weight)
     fits = (
         lax.axis_size("dp") % 2 == 0
+        and lax.axis_size("dp") > 2
         and hidden.shape[3] % 8 == 0
         and down_weight.shape[1] % 16 == 0
         and hidden.shape[4] % 128 == 0

time: 47.4 us -> 45.6 us (0.962)
  Pallas kernels: 46.6 us -> 44.8 us
    pallas_call x1, Pallas kernels: 45.3 us -> 43.4 us  [fused(): pl.pallas_call(functools.partial(kernel, window, shards, capacity, PIECES...]
where the time goes in v1:
time: 45.6 us; the launch traced here: 45.4 us
  Pallas kernels  44.8 us (98%)
  between operations  0.64 us (1%)
    pallas_call x1, Pallas kernels, fused(): pl.pallas_call(functools.partial(kernel, window, shards, capacity, PIECES...  43.4 us
    pallas_call x1, Pallas kernels, fused(): pl.pallas_call(write_out, out_shape=tuple((jax.ShapeDtypeStruct(a.shape,...  1.33 us

profile of v1, /device:TPU:0, one launch (start us, length us, event | category | flops | bytes accessed | tf_op | source)
XLA Modules:
  0.0 45.4 jit_solution(9553844138097436024)
XLA Ops:
  0.6 43.4 %shard_map.94 = (bf16[8,40,768]{2,1,0:T(8,128)(2,1)S(1)}, f32[192,2048]{1,0:T(8,128)S(1)}, f32[8,128]{1,0:T(8,128)S(1)}) custom-call(bf16[128,2048]{1,0:T(8,128)(2,1)} %token_hbm.1, f32[8,128]{1,0:T(8,128)} %bitcast.11, s32[8,128]{1,0:T(8,128)} %bitcast.12, s32[8,128]{1,0:T(8,128)} %bitcast.13, f32[8,128]{1,0:T(8,128)} %bitcast.14, ...), custom_call_target="tpu_custom_call" | custom-call | tf_op jit(solution)/shard_map/pallas_call | solution.py:335
  44.1 1.3 %shard_map.95 = (bf16[8,40,768]{2,1,0:T(8,128)(2,1)}, f32[192,2048]{1,0:T(8,128)}, f32[8,128]{1,0:T(8,128)}) custom-call(bf16[8,40,768]{2,1,0:T(8,128)(2,1)S(1)} %get-tuple-element.9.a, f32[192,2048]{1,0:T(8,128)S(1)} %get-tuple-element.10.b, f32[8,128]{1,0:T(8,128)S(1)} %get-tuple-element.11.c), custom_call_target="tpu_custom_call" | custom-call | tf_op jit(solution)/shard_map/pallas_call | solution.py:386

commit v2 on v1

--- a/solution.py
+++ b/solution.py
@@ -9,17 +9,23 @@
 
 MESH = pl.DeviceIdType.MESH
 PIECES = 8
-AHEAD = 3
+FIRST = 0
+LAST = 0
+AHEAD = 2
+NEAR_AHEAD = 4
+DIRECT_AHEAD = 3
+COLUMNS = 2
 
 
 def kernel(
-    window, shards, capacity, pieces, ahead,
+    window, shards, capacity, pieces, first, last, ahead, near_ahead, direct_ahead, columns,
     token_hbm, logits_hbm, chosen_hbm, slots_hbm, other_hbm, hidden_hbm, weight_ref,
     gradh_ref, down_ref, logit_ref,
     token_ref, logits_ref, chosen_ref, slots_ref, other_ref, hidden_ref,
     rsend, rrecv, msend, mrecv, wfull, padded, hturn, upward, own, csend, crecv, ysend, yrecv,
-    tsend, trecv, gates,
-    rs, rr, ms, mr, ws, wr, dr, fs, cs, cr, ys, yr, ts, tr, ls, lw,
+    tsend, trecv, gates, tin, fsend, lsend, fmeta, fplace, lplace,
+    rs, rr, ms, mr, ws, wr, dr, fs, cs, cr, ys, yr, ts, tr, ls, lw, go,
+    rf, ro, bs, br, bo, ps, pm, qs, qr,
 ):
     me = lax.axis_index("expert")
     place = lax.axis_index("dp")
@@ -39,10 +45,27 @@
                 where = where + (1 << bit) * (1 - 2 * (me // (1 << bit) % 2))
         return where
 
-    if window & (window - 1):
-        near = [lax.rem(me + step, window) for step in range(window)]
-    else:
-        near = [flipped(mask) for mask in (0, *range(window - 1, 0, -1))]
+    near = [flipped(mask) for mask in (0, *range(window - 1, 0, -1))]
+
+    level, column = me // columns, me % columns
+    half, members = level // 2, window // 2
+    base, far_base = half * members, (1 - half) * members
+    inner = (level + 1) // 2 % 2
+    side = level % 2
+    own_level = side * columns
+    beyond = (2 - half) * columns + column
+    inward = (1 + half) * columns + column
+    outward = half * 3 * columns + column
+    far_dests = [flipped(mask) for mask in range(window - 1, members - 1, -1)]
+    near_dests = [flipped(mask) for mask in range(members - 1, 0, -1)]
+    off_level = [flipped(mask) for mask in range(members - 1, columns - 1, -1)]
+    beside = [flipped(mask) for mask in range(columns - 1, 0, -1)]
+
+    relayed = pieces - first - last
+    end = first + relayed
+
+    def is_relayed(c):
+        return (c >= first) & (c < end)
 
     def other(step):
         return near[step]
@@ -82,11 +105,38 @@
         )
 
     barrier = pltpu.get_barrier_semaphore()
+
+    def signal(sem, target):
+        pl.semaphore_signal(sem, inc=1, device_id=target, device_id_type=MESH)
+
+    for step in range(1, chips):
+        signal(barrier, (me, chip_at(step) * 2 + 1))
+
+    @pl.when(core == 0)
+    def _():
+        signal(barrier, mate)
+
     for step in range(1, window):
-        pl.semaphore_signal(barrier, inc=1, device_id=(other(step), place), device_id_type=MESH)
-    for step in range(1, chips):
-        pl.semaphore_signal(barrier, inc=1, device_id=across(step), device_id_type=MESH)
-    pl.semaphore_signal(barrier, inc=1, device_id=mate, device_id_type=MESH)
+        signal(barrier, (other(step), chip * 2))
+
+    @pl.when(core == 1)
+    def _():
+        with jax.named_scope("w_near"):
+            pl.semaphore_wait(barrier, 2 * chips - 1)
+        signal(go, mate)
+
+    @pl.when(core == 0)
+    def _():
+        with jax.named_scope("w_near"):
+            pl.semaphore_wait(go, 1)
+
+    def launch_weights(c, carry):
+        for step in range(1, chips):
+            weight_copy(c, across(step), wr.at[c, step - 1]).start()
+        weight_copy(c, mate, dr.at[c]).start()
+        return carry
+
+    lax.fori_loop(0, pieces, launch_weights, 0)
 
     k = logit_ref.shape[0]
     for load in loads[:5]:
@@ -102,7 +152,7 @@
         here = live & (chosen == w)
         pos = jnp.sum(jnp.where(here, slots.astype(jnp.float32) + 1.0, 0.0), axis=0, keepdims=True) - 1.0
         gate = jnp.sum(jnp.where(here, sent_gate, 0.0), axis=0, keepdims=True)
-        line = lax.broadcasted_iota(jnp.int32, (8, tokens), 0)
+        line = lax.broadcasted_iota(jnp.int32, (2, tokens), 0)
         msend[w] = jnp.where(line == 0, pos, gate)
 
     slot_id = lax.broadcasted_iota(jnp.int32, (rows, tokens), 0).astype(jnp.float32)
@@ -110,20 +160,53 @@
     def spread(ref, w):
         return slot_id == ref[w, 0:1, :]
 
-    dispatch = jnp.concatenate(
-        [spread(msend, w).astype(jnp.float32) for w in range(window)], axis=0
-    ).astype(jnp.bfloat16)
-
-    def fill(c):
+    def placing(first):
+        return jnp.concatenate(
+            [spread(msend, first + w).astype(jnp.float32) for w in range(members)], axis=0
+        ).astype(jnp.bfloat16)
+
+    dispatch, far_dispatch = placing(base), placing(far_base)
+
+    def fill(c, matrix, first):
         lanes = pl.ds(pl.multiple_of(c * piece, piece), piece)
-        placed = jnp.dot(dispatch, token_ref[:, lanes], preferred_element_type=jnp.float32)
-        rsend[c] = placed.astype(jnp.bfloat16).reshape(window, rows, piece)
-
-    def row_copy(c, dest, source):
+        placed = jnp.dot(matrix, token_ref[:, lanes], preferred_element_type=jnp.float32)
+        rsend[c, pl.ds(first, members)] = placed.astype(jnp.bfloat16).reshape(members, rows, piece)
+
+    def block_copy(c, dest, slot, sem):
+        lanes = pl.ds(pl.multiple_of(c * piece, piece), piece)
+        return pltpu.make_async_remote_copy(
+            src_ref=token_ref.at[:, lanes], dst_ref=tin.at[c - first, slot],
+            send_sem=bs, recv_sem=sem.at[c - first],
+            device_id=(dest, place), device_id_type=MESH,
+        )
+
+    def pass_block(c):
+        return pltpu.make_async_remote_copy(
+            src_ref=tin.at[c - first, 2], dst_ref=tin.at[c - first, 1 - side],
+            send_sem=bs, recv_sem=br.at[c - first],
+            device_id=(beyond, place), device_id_type=MESH,
+        )
+
+    def far_meta(first, dest, slot):
+        return pltpu.make_async_remote_copy(
+            src_ref=msend.at[pl.ds(first, members)], dst_ref=fmeta.at[slot],
+            send_sem=qs, recv_sem=qr,
+            device_id=(dest, place), device_id_type=MESH,
+        )
+
+    def forward_copy(block, c, source, dest, sem):
+        return pltpu.make_async_remote_copy(
+            src_ref=block.at[pl.ds(0, capacity)],
+            dst_ref=rrecv.at[c, source, pl.ds(0, capacity)],
+            send_sem=sem, recv_sem=rr.at[c],
+            device_id=(dest, place), device_id_type=MESH,
+        )
+
+    def row_copy(c, dest, source, sem):
         return pltpu.make_async_remote_copy(
             src_ref=rsend.at[c, dest, pl.ds(0, capacity)],
             dst_ref=rrecv.at[c, source, pl.ds(0, capacity)],
-            send_sem=rs, recv_sem=rr.at[c],
+            send_sem=sem, recv_sem=rr.at[c],
             device_id=(dest, place), device_id_type=MESH,
         )
 
@@ -162,36 +245,75 @@
             device_id=across(step), device_id_type=MESH,
         )
 
-    fill(0)
-    pl.semaphore_wait(barrier, window - 1 + chips)
-
-    def launch_weights(c, carry):
-        for step in range(1, chips):
-            weight_copy(c, across(step), wr.at[c, step - 1]).start()
-        weight_copy(c, mate, dr.at[c]).start()
-        return carry
-
-    lax.fori_loop(0, pieces, launch_weights, 0)
+    fill(0, dispatch, base)
+    for c in range(first):
+        fill(c, far_dispatch, far_base)
+
+    @pl.when(core == 0)
+    def _():
+        with jax.named_scope("w_bar"):
+            pl.semaphore_wait(barrier, 2 * (window - 1))
+        signal(go, mate)
+
+    @pl.when(core == 1)
+    def _():
+        with jax.named_scope("w_bar"):
+            pl.semaphore_wait(go, 1)
+
+
+    @pl.when(inner == 1)
+    def _():
+        far_meta(far_base, beyond, side).start()
+
+    @pl.when(inner == 0)
+    def _():
+        far_meta(far_base, beyond, side).start()
+        far_meta(base, inward, 2).start()
 
     for step in range(1, window):
         meta_copy(other(step), me).start()
 
-    def send_rows(c):
-        for step in range(1, window):
-            row_copy(c, other(step), me).start()
+    def send_near(c):
+        for dest in beside:
+            row_copy(c, dest, me, rs).start()
+
+        @pl.when((inner == 1) | jnp.logical_not(is_relayed(c)))
+        def _():
+            for dest in off_level:
+                row_copy(c, dest, me, ro).start()
+
+    def send_far(c):
+        for dest in far_dests:
+            row_copy(c, dest, me, rf).start()
+
+    for c in range(first):
+        send_far(c)
+        send_near(c)
+
+    @pl.when(inner == 1)
+    def _():
+        for c in range(first, first + ahead):
+            block_copy(c, beyond, side, br).start()
+
+    @pl.when(inner == 0)
+    def _():
+        for c in range(first, end):
+            block_copy(c, inward, 2, bo).start()
 
     def launch(c, carry):
-        @pl.when(c < ahead)
-        def _():
-            send_rows(c)
+        @pl.when((c >= first) & ((inner == 0) & (c < end) | (inner == 1) & (c < first + near_ahead)))
+        def _():
+            send_near(c)
 
         @pl.when(c + 1 < pieces)
         def _():
-            fill(c + 1)
+            fill(c + 1, dispatch, base)
 
         return carry
 
     lax.fori_loop(0, pieces, launch, 0)
+    for c in range(end, pieces):
+        fill(c, far_dispatch, far_base)
 
     mrecv[me] = msend[me]
     for c in range(pieces):
@@ -215,6 +337,65 @@
             jnp.where(spread(mrecv, s), mrecv[s, 1:2, :], 0.0), axis=1, keepdims=True
         )
 
+    def pump(c):
+        with jax.named_scope("w_pump"):
+            block = tin.at[c - first, 2]
+            pltpu.make_async_copy(block, block, bo.at[c - first]).wait()
+        pass_block(c).start()
+
+    def relay(c):
+        with jax.named_scope("w_relay"):
+            blocks = tin.at[c - first, pl.ds(0, 2)]
+            pltpu.make_async_copy(blocks, blocks, br.at[c - first]).wait()
+
+        @pl.when(c + ahead < end)
+        def _():
+            block_copy(c + ahead, beyond, side, br).start()
+            pump(c + ahead)
+
+        if last:
+            @pl.when((c + ahead >= end) & (c + ahead < pieces))
+            def _():
+                send_far(c + ahead)
+
+        sources = [((1 - half) * 2 + i) * columns + column for i in range(2)]
+        for i in range(2):
+            placed = jnp.dot(fplace[i], tin[c - first, i], preferred_element_type=jnp.float32)
+            fsend[c - first, i] = placed.astype(jnp.bfloat16).reshape(members, rows, piece)
+        placed = jnp.dot(lplace[...], tin[c - first, 2], preferred_element_type=jnp.float32)
+        lsend[c - first] = placed.astype(jnp.bfloat16).reshape(columns, rows, piece)
+        for dest in near_dests:
+            for i in range(2):
+                forward_copy(fsend.at[c - first, i, dest - base], c, sources[i], dest, ps).start()
+        for dest in beside:
+            forward_copy(lsend.at[c - first, dest % columns], c, outward, dest, pm).start()
+
+        @pl.when(c + near_ahead < pieces)
+        def _():
+            send_near(c + near_ahead)
+
+        for i in range(2):
+            rrecv[c, sources[i], 0:capacity] = fsend[c - first, i, me - base, 0:capacity]
+        rrecv[c, outward, 0:capacity] = lsend[c - first, column, 0:capacity]
+
+    @pl.when(inner == 1)
+    def _():
+        pltpu.make_async_copy(fmeta, fmeta, qr).wait()
+        for i in range(2):
+            fplace[i] = jnp.concatenate(
+                [(slot_id == fmeta[i, w, 0:1, :]).astype(jnp.float32) for w in range(members)], axis=0
+            ).astype(jnp.bfloat16)
+        lplace[...] = jnp.concatenate(
+            [
+                (slot_id == fmeta[2, own_level + w, 0:1, :]).astype(jnp.float32)
+                for w in range(columns)
+            ],
+            axis=0,
+        ).astype(jnp.bfloat16)
+        for c in range(first, first + ahead):
+            pump(c)
+        relay(first)
+
     def combine(c):
         lanes = pl.ds(pl.multiple_of(c * piece, piece), piece)
         with jax.named_scope("w_core"):
@@ -226,6 +407,10 @@
         down_ref[:, lanes] = own[c, chip] + crecv[c, chip].astype(jnp.float32)
 
     def finish(c, carry):
+        @pl.when((inner == 1) & (c + 1 > first) & (c + 1 < end))
+        def _():
+            relay(c + 1)
+
         @pl.when(c > 0)
         def _():
             combine(c - 1)
@@ -234,13 +419,28 @@
             came = lax.rem(chip + chips - step, chips) * 2 + core
             weight_copy(c, mate, wr.at[c, step - 1]).wait_recv()
             pass_copy(c, came).start()
-        came_rows = rrecv.at[c, pl.ds(0, window - 1), pl.ds(0, capacity)]
-        with jax.named_scope("w_rows"):
-            pltpu.make_async_copy(came_rows, came_rows, rr.at[c]).wait()
-
-        @pl.when(c + ahead < pieces)
-        def _():
-            send_rows(c + ahead)
+        def rows_in(count):
+            came_rows = rrecv.at[c, pl.ds(0, count), pl.ds(0, capacity)]
+            with jax.named_scope("w_rows"):
+                pltpu.make_async_copy(came_rows, came_rows, rr.at[c]).wait()
+
+        kept = (inner == 1) & is_relayed(c)
+
+        @pl.when(kept)
+        def _():
+            rows_in(window - 4)
+
+        @pl.when(jnp.logical_not(kept))
+        def _():
+            rows_in(window - 1)
+
+        if last:
+            later = c + direct_ahead
+
+            @pl.when((inner == 0) & (later >= end) & (later < pieces))
+            def _():
+                send_far(later)
+                send_near(later)
 
         got = rrecv[c].reshape(slots_all, piece)
         scaled = (gates[...].reshape(slots_all, 1) * got.astype(jnp.float32)).astype(jnp.bfloat16)
@@ -267,7 +467,7 @@
         up = upward[s * rows : (s + 1) * rows]
         score = jnp.sum(padded[s].astype(jnp.float32) * up, axis=1, keepdims=True)
         back = jnp.sum(jnp.where(spread(mrecv, s), score, 0.0), axis=0, keepdims=True)
-        tsend[s] = jnp.broadcast_to(back, (8, tokens))
+        tsend[s] = back
     for step in range(1, window):
         score_copy(other(step), me).start()
     trecv[me] = tsend[me]
@@ -290,7 +490,26 @@
     sent(wfull.at[:, pl.ds(0, chips)], ws)
     sent(wfull.at[:, pl.ds(0, chips - 1)], fs)
     sent(csend, cs)
-    sent(rsend.at[:, pl.ds(0, window - 1), pl.ds(0, capacity)], rs)
+    direct = first + last
+    sent(rsend.at[:, pl.ds(0, columns - 1), pl.ds(0, capacity)], rs)
+    if direct:
+        sent(rsend.at[pl.ds(0, direct), pl.ds(0, members), pl.ds(0, capacity)], rf)
+
+    @pl.when(inner == 1)
+    def _():
+        sent(rsend.at[:, pl.ds(0, members - columns), pl.ds(0, capacity)], ro)
+        sent(tin.at[:, pl.ds(0, 2)], bs)
+        sent(msend.at[pl.ds(0, members)], qs)
+        sent(fsend.at[:, :, pl.ds(0, members - 1), pl.ds(0, capacity)], ps)
+        sent(lsend.at[:, pl.ds(0, columns - 1), pl.ds(0, capacity)], pm)
+
+    @pl.when(inner == 0)
+    def _():
+        if direct:
+            sent(rsend.at[pl.ds(0, direct), pl.ds(0, members - columns), pl.ds(0, capacity)], ro)
+        sent(tin.at[:, 0], bs)
+        sent(msend, qs)
+
     settle(msend, ms)
     lax.fori_loop(0, pieces - 1, collect, 0)
 
@@ -333,7 +552,10 @@
     bf, f32, dma = jnp.bfloat16, jnp.float32, pltpu.SemaphoreType.DMA
     slots_all = window * rows
     gradh, down, turned = pl.pallas_call(
-        functools.partial(kernel, window, shards, capacity, PIECES, min(AHEAD, PIECES)),
+        functools.partial(
+            kernel, window, shards, capacity, PIECES, FIRST, LAST, AHEAD, NEAR_AHEAD, DIRECT_AHEAD,
+            COLUMNS,
+        ),
         out_shape=(
             jax.ShapeDtypeStruct((window, capacity, hidden_units), bf),
             jax.ShapeDtypeStruct((shard_rows, width), f32),
@@ -350,8 +572,8 @@
             pltpu.VMEM((window, capacity, hidden_units), bf),
             pltpu.VMEM((PIECES, window, rows, piece), bf),
             pltpu.VMEM((PIECES, window, rows, piece), bf),
-            pltpu.VMEM((window, 8, tokens), f32),
-            pltpu.VMEM((window, 8, tokens), f32),
+            pltpu.VMEM((window, 2, tokens), f32),
+            pltpu.VMEM((window, 2, tokens), f32),
             pltpu.VMEM((PIECES, shards, shard_rows, piece), bf),
             pltpu.VMEM((window, rows, hidden_units), bf),
             pltpu.VMEM((shards, shard_rows, slots_all), bf),
@@ -361,9 +583,15 @@
             pltpu.VMEM((PIECES, chips, shard_rows, piece), bf),
             pltpu.VMEM((PIECES, chips - 1, shard_rows, piece), bf),
             pltpu.VMEM((PIECES, chips - 1, shard_rows, piece), bf),
-            pltpu.VMEM((window, 8, tokens), f32),
-            pltpu.VMEM((window, 8, tokens), f32),
+            pltpu.VMEM((window, 1, tokens), f32),
+            pltpu.VMEM((window, 1, tokens), f32),
             pltpu.VMEM((window, rows, 1), f32),
+            pltpu.VMEM((PIECES - FIRST - LAST, 3, tokens, piece), bf),
+            pltpu.VMEM((PIECES - FIRST - LAST, 2, window // 2, rows, piece), bf),
+            pltpu.VMEM((PIECES - FIRST - LAST, COLUMNS, rows, piece), bf),
+            pltpu.VMEM((3, window // 2, 2, tokens), f32),
+            pltpu.VMEM((2, window // 2 * rows, tokens), bf),
+            pltpu.VMEM((COLUMNS * rows, tokens), bf),
             dma, dma((PIECES,)),
             dma, dma,
             dma, dma((PIECES, chips - 1)), dma((PIECES,)),
@@ -371,7 +599,8 @@
             dma, dma((PIECES,)),
             dma, dma((PIECES,)),
             dma, dma,
-            dma((6,)), dma,
+            dma((6,)), dma, pltpu.SemaphoreType.REGULAR,
+            dma, dma, dma, dma((PIECES - FIRST - LAST,)), dma((PIECES - FIRST - LAST,)), dma, dma, dma, dma,
         ],
         compiler_params=pltpu.CompilerParams(
             collective_id=0, has_side_effects=True, vmem_limit_bytes=48 * 1024 * 1024
@@ -460,6 +689,7 @@
     fits = (
         lax.axis_size("dp") % 2 == 0
         and lax.axis_size("dp") > 2
+        and lax.axis_size("expert") == 4 * COLUMNS
         and hidden.shape[3] % 8 == 0
         and down_weight.shape[1] % 16 == 0
         and hidden.shape[4] % 128 == 0

time: 45.6 us -> 44.4 us (0.974)
  Pallas kernels: 44.8 us -> 43.6 us
    pallas_call x1, Pallas kernels: 43.4 us -> 42.2 us  [fused(): pl.pallas_call(functools.partial(kernel, window, shards, capacity, PIECES...]
where the time goes in v2:
time: 44.4 us; the launch traced here: 44.2 us
  Pallas kernels  43.6 us (98%)
  between operations  0.64 us (1%)
    pallas_call x1, Pallas kernels, fused(): pl.pallas_call(functools.partial(kernel, window, shards, capacity, PIECES...  42.2 us
    pallas_call x1, Pallas kernels, fused(): pl.pallas_call(write_out, out_shape=tuple((jax.ShapeDtypeStruct(a.shape,...  1.33 us

profile of v2, /device:TPU:0, one launch (start us, length us, event | category | flops | bytes accessed | tf_op | source)
XLA Modules:
  0.0 44.2 jit_solution(7276753724387423419)
XLA Ops:
  0.6 42.2 %shard_map.94 = (bf16[8,40,768]{2,1,0:T(8,128)(2,1)S(1)}, f32[192,2048]{1,0:T(8,128)S(1)}, f32[8,128]{1,0:T(8,128)S(1)}) custom-call(bf16[128,2048]{1,0:T(8,128)(2,1)} %token_hbm.1, f32[8,128]{1,0:T(8,128)} %bitcast.11, s32[8,128]{1,0:T(8,128)} %bitcast.12, s32[8,128]{1,0:T(8,128)} %bitcast.13, f32[8,128]{1,0:T(8,128)} %bitcast.14, ...), custom_call_target="tpu_custom_call" | custom-call | tf_op jit(solution)/shard_map/pallas_call | solution.py:554
  42.9 1.3 %shard_map.95 = (bf16[8,40,768]{2,1,0:T(8,128)(2,1)}, f32[192,2048]{1,0:T(8,128)}, f32[8,128]{1,0:T(8,128)}) custom-call(bf16[8,40,768]{2,1,0:T(8,128)(2,1)S(1)} %get-tuple-element.9.a, f32[192,2048]{1,0:T(8,128)S(1)} %get-tuple-element.10.b, f32[8,128]{1,0:T(8,128)S(1)} %get-tuple-element.11.c), custom_call_target="tpu_custom_call" | custom-call | tf_op jit(solution)/shard_map/pallas_call | solution.py:615

commit v3 on v1

v3 whole, which is shorter than its diff:
```python
import functools

import jax
import jax.numpy as jnp
from jax import lax
from jax.experimental import pallas as pl
from jax.experimental.pallas import tpu as pltpu
from jax.sharding import PartitionSpec as P

MESH = pl.DeviceIdType.MESH
PIECE = 256
SMALL = 128
AHEAD = 3
NEAR_AHEAD = 7
NEAR_LEAD = 3
RELAY_AHEAD = 2
PASS_AHEAD = 1
COLUMNS = 2


class Part:
    def __init__(self, p, small, count, width):
        self.p = p
        self.small = small
        if small:
            self.index, self.size = p // (count - 1), SMALL
            start = self.index * (width - SMALL)
        else:
            self.index, self.size = p - 1, PIECE
            start = SMALL + self.index * PIECE
        self.lanes = pl.ds(pl.multiple_of(start, 128), self.size)

    def of(self, pair):
        return pair[self.small].at[self.index]


def kernel(
    window, shards, capacity, ahead, near_ahead, near_lead, relay_ahead, pass_ahead, columns,
    token_hbm, logits_hbm, chosen_hbm, slots_hbm, other_hbm, hidden_hbm, weight_ref,
    gradh_ref, down_ref, logit_ref,
    token_ref, logits_ref, chosen_ref, slots_ref, other_ref, hidden_ref,
    msend, mrecv, padded, hturn, upward, tsend, trecv, gates, fmeta, fplace, lplace,
    rsend_b, rrecv_b, wfull_b, own_b, csend_b, crecv_b, ysend_b, yrecv_b, tin_b, fsend_b, lsend_b,
    rsend_s, rrecv_s, wfull_s, own_s, csend_s, crecv_s, ysend_s, yrecv_s, tin_s, fsend_s, lsend_s,
    rr, wr, dr, cr, yr, br, bo, mr, tr, qr, ws, cs, rs, ls, lh, lw, go,
):
    rsend, rrecv, wfull = (rsend_b, rsend_s), (rrecv_b, rrecv_s), (wfull_b, wfull_s)
    own, csend, crecv = (own_b, own_s), (csend_b, csend_s), (crecv_b, crecv_s)
    ysend, yrecv, tin = (ysend_b, ysend_s), (yrecv_b, yrecv_s), (tin_b, tin_s)
    fsend, lsend = (fsend_b, fsend_s), (lsend_b, lsend_s)
    me = lax.axis_index("expert")
    place = lax.axis_index("dp")
    chip, core = place // 2, place % 2
    chips = shards // 2
    mate = (me, chip * 2 + 1 - core)
    tokens, width = token_ref.shape
    count = rsend_b.shape[0] + 2
    rows = rsend_b.shape[2]
    slots_all = window * rows
    shard_rows, hidden_units = weight_ref.shape[0], hidden_ref.shape[2]

    def at(p, act):
        if isinstance(p, int):
            act(Part(p, p in (0, count - 1), count, width))
            return
        small = (p == 0) | (p == count - 1)

        @pl.when(small)
        def _():
            act(Part(p, True, count, width))

        @pl.when(jnp.logical_not(small))
        def _():
            act(Part(p, False, count, width))

    def flipped(mask):
        where = me
        for bit in range(window.bit_length() - 1):
            if mask >> bit & 1:
                where = where + (1 << bit) * (1 - 2 * (me // (1 << bit) % 2))
        return where

    level, column = me // columns, me % columns
    half, members = level // 2, window // 2
    base, far_base = half * members, (1 - half) * members
    inner = (level + 1) // 2 % 2
    side = level % 2
    own_level = side * columns
    beyond = (2 - half) * columns + column
    inward = (1 + half) * columns + column
    outward = half * 3 * columns + column
    others = [flipped(mask) for mask in range(window - 1, 0, -1)]
    near_dests = [flipped(mask) for mask in range(members - 1, 0, -1)]
    off_level = [flipped(mask) for mask in range(members - 1, columns - 1, -1)]
    beside = [flipped(mask) for mask in range(columns - 1, 0, -1)]

    def arrived(ref, sem):
        pltpu.make_async_copy(ref, ref, sem).wait()

    def settle(buffer, sem):
        arrived(buffer.at[pl.ds(0, window - 1)], sem)

    def chip_at(step):
        return lax.rem(chip + step, chips)

    def across(step):
        return (me, chip_at(step) * 2 + core)

    def remote(src, dst, send, recv, target):
        return pltpu.make_async_remote_copy(
            src_ref=src, dst_ref=dst, send_sem=send, recv_sem=recv,
            device_id=target, device_id_type=MESH,
        )

    def signal(sem, target):
        pl.semaphore_signal(sem, inc=1, device_id=target, device_id_type=MESH)

    loads = [
        pltpu.make_async_copy(src, dst, ls)
        for src, dst in (
            (chosen_hbm, chosen_ref), (slots_hbm, slots_ref), (token_hbm, token_ref),
            (logits_hbm, logits_ref), (other_hbm, other_ref),
        )
    ]
    load_hidden = pltpu.make_async_copy(hidden_hbm, hidden_ref, lh)
    for load in loads:
        load.start()
    load_hidden.start()

    barrier = pltpu.get_barrier_semaphore()
    for step in range(1, chips):
        signal(barrier, (me, chip_at(step) * 2 + 1))

    signal(barrier, mate)
    for dest in others:
        signal(barrier, (dest, chip * 2))

    def weight_copy(part, target, sem):
        return remote(weight_ref.at[:, part.lanes], part.of(wfull).at[place], ws, sem, target)

    def launch_weights(p, carry):
        def start(part):
            for step in range(1, chips):
                weight_copy(part, across(step), wr.at[p, step - 1]).start()
            weight_copy(part, mate, dr.at[p]).start()

        at(p, start)
        return carry

    @pl.when(core == 1)
    def _():
        with jax.named_scope("w_near"):
            pl.semaphore_wait(barrier, 2 * chips - 1)
        signal(go, mate)
        lax.fori_loop(0, count, launch_weights, 0)

    k = logit_ref.shape[0]
    for load in loads:
        load.wait()
    raised = jnp.exp(logits_ref[...])
    gating = raised / jnp.sum(raised, axis=0, keepdims=True)
    sent_gate = gating.astype(jnp.bfloat16).astype(jnp.float32)
    chosen = chosen_ref[...]
    slots = slots_ref[...]
    outside = jnp.where(chosen >= window, other_ref[...], 0.0)
    live = slots < capacity
    for w in range(window):
        here = live & (chosen == w)
        pos = jnp.sum(jnp.where(here, slots.astype(jnp.float32) + 1.0, 0.0), axis=0, keepdims=True) - 1.0
        gate = jnp.sum(jnp.where(here, sent_gate, 0.0), axis=0, keepdims=True)
        line = lax.broadcasted_iota(jnp.int32, (2, tokens), 0)
        msend[w] = jnp.where(line == 0, pos, gate)

    slot_id = lax.broadcasted_iota(jnp.int32, (rows, tokens), 0).astype(jnp.float32)

    def spread(ref, w):
        return slot_id == ref[w, 0:1, :]

    def placing(lines):
        return jnp.concatenate(
            [(slot_id == line).astype(jnp.float32) for line in lines], axis=0
        ).astype(jnp.bfloat16)

    dispatch = placing([msend[base + w, 0:1, :] for w in range(members)])

    def place_rows(matrix, block, experts):
        placed = jnp.dot(matrix, block, preferred_element_type=jnp.float32)
        return placed.astype(jnp.bfloat16).reshape(experts, rows, block.shape[1])

    def fill(part):
        part.of(rsend)[pl.ds(base, members)] = place_rows(dispatch, token_ref[:, part.lanes], members)

    def row_copy(part, dest):
        held = pl.ds(0, capacity)
        return remote(
            part.of(rsend).at[dest, held], part.of(rrecv).at[me, held], rs, rr.at[part.p], (dest, place)
        )

    def forward_copy(block, part, source, dest):
        held = pl.ds(0, capacity)
        return remote(
            block.at[held], part.of(rrecv).at[source, held], rs, rr.at[part.p], (dest, place)
        )

    def block_copy(part, dest, slot, sem):
        return remote(
            token_ref.at[:, part.lanes], part.of(tin).at[slot], rs, sem.at[part.p], (dest, place)
        )

    def pass_block(part):
        return remote(
            part.of(tin).at[2], part.of(tin).at[1 - side], rs, br.at[part.p], (beyond, place)
        )

    def relay_meta(first, dest, slot):
        return remote(msend.at[pl.ds(first, members)], fmeta.at[slot], rs, qr, (dest, place))

    def meta_copy(dest):
        return remote(msend.at[dest], mrecv.at[me], rs, mr, (dest, place))

    def score_copy(dest):
        return remote(tsend.at[dest], trecv.at[me], rs, tr, (dest, place))

    def pass_copy(part, slot):
        shard = part.of(wfull).at[slot]
        return remote(shard, shard, ws, dr.at[part.p], mate)

    def core_copy(part):
        return remote(part.of(csend), part.of(crecv), cs, cr.at[part.p], mate)

    def sum_copy(part, step):
        return remote(
            part.of(ysend).at[step - 1], part.of(yrecv).at[step - 1], cs, yr.at[part.p], across(step)
        )

    at(0, fill)

    @pl.when(core == 0)
    def _():
        with jax.named_scope("w_bar"):
            pl.semaphore_wait(barrier, 2 * (window - 1) + 1)
        signal(go, mate)

    @pl.when(core == 1)
    def _():
        with jax.named_scope("w_bar"):
            pl.semaphore_wait(go, 1)

    relay_meta(far_base, beyond, side).start()

    @pl.when(inner == 0)
    def _():
        relay_meta(base, inward, 2).start()

    for dest in others:
        meta_copy(dest).start()

    @pl.when(inner == 1)
    def _():
        for p in range(ahead):
            at(p, lambda part: block_copy(part, beyond, side, br).start())

    @pl.when(inner == 0)
    def _():
        for p in range(count):
            at(p, lambda part: block_copy(part, inward, 2, bo).start())

    @pl.when(core == 0)
    def _():
        with jax.named_scope("w_near"):
            pl.semaphore_wait(go, 1)
        lax.fori_loop(0, count, launch_weights, 0)

    def send_near(part):
        for dest in beside:
            row_copy(part, dest).start()

        @pl.when(inner == 1)
        def _():
            for dest in off_level:
                row_copy(part, dest).start()

    def launch(p, carry):
        @pl.when((inner == 0) | (p < near_ahead))
        def _():
            at(p, send_near)

        @pl.when(p + 1 < count)
        def _():
            at(p + 1, fill)

        return carry

    lax.fori_loop(0, count, launch, 0)

    keeps = []

    def keep_own(part):
        part.of(rrecv)[me, 0:capacity] = part.of(rsend)[me, 0:capacity]
        if rows > capacity:
            part.of(rrecv)[:, capacity:rows] = jnp.zeros(
                (window, rows - capacity, part.size), jnp.bfloat16
            )
        keeps.append(
            pltpu.make_async_copy(weight_ref.at[:, part.lanes], part.of(wfull).at[place], lw)
        )
        keeps[-1].start()

    mrecv[me] = msend[me]
    for p in range(count):
        at(p, keep_own)
    load_hidden.wait()
    padded[:, 0:capacity] = hidden_ref[...]
    if rows > capacity:
        padded[:, capacity:rows] = jnp.zeros((window, rows - capacity, hidden_units), jnp.bfloat16)
    flat = padded[...].reshape(slots_all, hidden_units)
    hturn[...] = flat.T.reshape(shards, shard_rows, slots_all)
    upward[...] = jnp.zeros_like(upward)
    for keep in keeps:
        keep.wait()

    settle(mrecv, mr)
    for s in range(window):
        gates[s] = jnp.sum(
            jnp.where(spread(mrecv, s), mrecv[s, 1:2, :], 0.0), axis=1, keepdims=True
        )

    def pump(part):
        with jax.named_scope("w_pump"):
            arrived(part.of(tin).at[2], bo.at[part.p])
        pass_block(part).start()

    def advance(part):
        block_copy(part, beyond, side, br).start()
        pump(part)

    def relay(part):
        blocks = part.of(tin)
        with jax.named_scope("w_relay"):
            arrived(blocks.at[pl.ds(0, 2)], br.at[part.p])

        @pl.when(part.p + ahead < count)
        def _():
            at(part.p + ahead, advance)

        placed, local = part.of(fsend), part.of(lsend)
        sources = [((1 - half) * 2 + i) * columns + column for i in range(2)]
        for i in range(2):
            placed[i] = place_rows(fplace[i], blocks[i], members)
        local[...] = place_rows(lplace[...], blocks[2], columns)
        for dest in near_dests:
            for i in range(2):
                forward_copy(placed.at[i, dest - base], part, sources[i], dest).start()
        for dest in beside:
            forward_copy(local.at[dest % columns], part, outward, dest).start()

        nearer = part.p + near_lead

        @pl.when((nearer >= near_ahead) & (nearer < count))
        def _():
            at(nearer, send_near)

        for i in range(2):
            part.of(rrecv)[sources[i], 0:capacity] = placed[i, me - base, 0:capacity]
        part.of(rrecv)[outward, 0:capacity] = local[column, 0:capacity]

    @pl.when(inner == 1)
    def _():
        arrived(fmeta, qr)
        for i in range(2):
            fplace[i] = placing([fmeta[i, w, 0:1, :] for w in range(members)])
        lplace[...] = placing([fmeta[2, own_level + w, 0:1, :] for w in range(columns)])
        for p in range(ahead):
            at(p, pump)
        for p in range(relay_ahead):
            at(p, relay)

    def combine(part):
        mine, came = part.of(own), part.of(crecv)
        with jax.named_scope("w_core"):
            core_copy(part).wait_recv()
        for step in range(1, chips):
            to = chip_at(step)
            part.of(ysend)[step - 1] = (mine[to] + came[to].astype(jnp.float32)).astype(jnp.bfloat16)
            sum_copy(part, step).start()
        down_ref[:, part.lanes] = mine[chip] + came[chip].astype(jnp.float32)

    def pass_weights(part):
        for step in range(1, chips):
            came = lax.rem(chip + chips - step, chips) * 2 + core
            weight_copy(part, mate, wr.at[part.p, step - 1]).wait_recv()
            pass_copy(part, came).start()

    for p in range(pass_ahead):
        at(p, pass_weights)

    def work(part):
        p = part.p

        def rows_in(remote_rows):
            with jax.named_scope("w_rows"):
                arrived(part.of(rrecv).at[pl.ds(0, remote_rows), pl.ds(0, capacity)], rr.at[p])

        @pl.when(inner == 1)
        def _():
            rows_in(window - 4)

        @pl.when(inner == 0)
        def _():
            rows_in(window - 1)

        got = part.of(rrecv)[...].reshape(slots_all, part.size)
        scaled = (gates[...].reshape(slots_all, 1) * got.astype(jnp.float32)).astype(jnp.bfloat16)
        for h in range(chips):
            part.of(csend)[h] = jnp.dot(
                hturn[2 * h + 1 - core], scaled, preferred_element_type=jnp.float32
            ).astype(jnp.bfloat16)
        core_copy(part).start()
        for h in range(chips):
            part.of(own)[h] = jnp.dot(
                hturn[2 * h + core], scaled, preferred_element_type=jnp.float32
            )
        with jax.named_scope("w_mate"):
            arrived(part.of(wfull).at[pl.ds(0, chips)], dr.at[p])
        weights = part.of(wfull)[...].reshape(hidden_units, part.size)
        upward[...] += lax.dot_general(
            got, weights, (((1,), (1,)), ((), ())), preferred_element_type=jnp.float32
        )

    def finish(p, carry):
        @pl.when((inner == 1) & (p + relay_ahead < count))
        def _():
            at(p + relay_ahead, relay)

        @pl.when(p > 0)
        def _():
            at(p - 1, combine)

        @pl.when(p + pass_ahead < count)
        def _():
            at(p + pass_ahead, pass_weights)

        at(p, work)
        return carry

    lax.fori_loop(0, count, finish, 0)
    def score_slots(dest):
        up = upward[pl.ds(pl.multiple_of(dest * rows, 16), rows)]
        score = jnp.sum(padded[dest].astype(jnp.float32) * up, axis=1, keepdims=True)
        tsend[dest] = jnp.sum(jnp.where(spread(mrecv, dest), score, 0.0), axis=0, keepdims=True)

    for dest in others[:members]:
        score_slots(dest)
        score_copy(dest).start()
    at(count - 1, combine)
    for dest in others[members:]:
        score_slots(dest)
        score_copy(dest).start()
    score_slots(me)
    trecv[me] = tsend[me]
    for s in range(window):
        up = upward[s * rows : s * rows + capacity]
        gradh_ref[s] = (gates[s, 0:capacity] * up).astype(jnp.bfloat16)

    def collect(part):
        with jax.named_scope("w_sum"):
            arrived(part.of(yrecv), yr.at[part.p])
        for step in range(1, chips):
            down_ref[:, part.lanes] += part.of(yrecv)[step - 1].astype(jnp.float32)

    held = pl.ds(0, capacity)
    for kind in range(2):
        arrived(wfull[kind].at[:, pl.ds(0, chips)], ws)
        arrived(wfull[kind].at[:, pl.ds(0, chips - 1)], ws)
        arrived(csend[kind], cs)
        arrived(rsend[kind].at[:, pl.ds(0, columns - 1), held], rs)

    @pl.when(inner == 1)
    def _():
        for kind in range(2):
            arrived(rsend[kind].at[:, pl.ds(0, members - columns), held], rs)
            arrived(tin[kind].at[:, pl.ds(0, 2)], rs)
            arrived(fsend[kind].at[:, :, pl.ds(0, members - 1), held], rs)
            arrived(lsend[kind].at[:, pl.ds(0, columns - 1), held], rs)
        arrived(msend.at[pl.ds(0, members)], rs)

    @pl.when(inner == 0)
    def _():
        for kind in range(2):
            arrived(tin[kind].at[:, 0], rs)
        arrived(msend, rs)

    settle(msend, rs)

    def collect_next(p, carry):
        at(p, collect)
        return carry

    lax.fori_loop(0, count - 1, collect_next, 0)

    with jax.named_scope("w_scores"):
        settle(trecv, tr)
    token_scores = jnp.zeros((k, tokens), jnp.float32)
    for w in range(window):
        token_scores = jnp.where(chosen == w, trecv[w], token_scores)
    scores_all = jnp.where(live, token_scores, outside)
    mean_score = jnp.sum(gating * scores_all, axis=0, keepdims=True)
    logit_ref[...] = gating * (scores_all - mean_score)
    settle(tsend, rs)

    at(count - 1, collect)
    for kind in range(2):
        arrived(ysend[kind], cs)


def write_out(a, b, c, a_out, b_out, c_out, sems):
    copies = [
        pltpu.make_async_copy(src, dst, sems.at[i])
        for i, (src, dst) in enumerate(((b, b_out), (a, a_out), (c, c_out)))
    ]
    for copy in copies:
        copy.start()
    for copy in copies:
        copy.wait()


def fused(grad_output, logits, chosen, slots, other_scores, hidden, down_weight):
    window = lax.axis_size("expert")
    shards = lax.axis_size("dp")
    capacity, hidden_units = hidden.shape[3], hidden.shape[4]
    tokens, width = grad_output.shape
    k = logits.shape[1]
    shard_rows = down_weight.shape[1]
    rows = -(-capacity // 16) * 16
    chips = shards // 2
    big = (width - 2 * SMALL) // PIECE
    count = big + 2
    vmem = pl.BlockSpec(memory_space=pltpu.VMEM)
    hbm = pl.BlockSpec(memory_space=pltpu.HBM)
    bf, f32, dma = jnp.bfloat16, jnp.float32, pltpu.SemaphoreType.DMA
    slots_all = window * rows

    def per_piece(pieces, lanes):
        return [
            pltpu.VMEM((pieces, *shape, lanes), dtype)
            for shape, dtype in (
                ((window, rows), bf),
                ((window, rows), bf),
                ((shards, shard_rows), bf),
                ((chips, shard_rows), f32),
                ((chips, shard_rows), bf),
                ((chips, shard_rows), bf),
                ((chips - 1, shard_rows), bf),
                ((chips - 1, shard_rows), bf),
                ((3, tokens), bf),
                ((2, window // 2, rows), bf),
                ((COLUMNS, rows), bf),
            )
        ]

    gradh, down, turned = pl.pallas_call(
        functools.partial(kernel, window, shards, capacity, AHEAD, NEAR_AHEAD, NEAR_LEAD, RELAY_AHEAD, PASS_AHEAD, COLUMNS),
        out_shape=(
            jax.ShapeDtypeStruct((window, capacity, hidden_units), bf),
            jax.ShapeDtypeStruct((shard_rows, width), f32),
            jax.ShapeDtypeStruct((k, tokens), f32),
        ),
        in_specs=[hbm] * 7,
        out_specs=(vmem,) * 3,
        scratch_shapes=[
            pltpu.VMEM((tokens, width), bf),
            pltpu.VMEM((k, tokens), f32),
            pltpu.VMEM((k, tokens), jnp.int32),
            pltpu.VMEM((k, tokens), jnp.int32),
            pltpu.VMEM((k, tokens), f32),
            pltpu.VMEM((window, capacity, hidden_units), bf),
            pltpu.VMEM((window, 2, tokens), f32),
            pltpu.VMEM((window, 2, tokens), f32),
            pltpu.VMEM((window, rows, hidden_units), bf),
            pltpu.VMEM((shards, shard_rows, slots_all), bf),
            pltpu.VMEM((slots_all, hidden_units), f32),
            pltpu.VMEM((window, 1, tokens), f32),
            pltpu.VMEM((window, 1, tokens), f32),
            pltpu.VMEM((window, rows, 1), f32),
            pltpu.VMEM((3, window // 2, 2, tokens), f32),
            pltpu.VMEM((2, window // 2 * rows, tokens), bf),
            pltpu.VMEM((COLUMNS * rows, tokens), bf),
            *per_piece(big, PIECE),
            *per_piece(2, SMALL),
            dma((count,)), dma((count, chips - 1)), dma((count,)), dma((count,)), dma((count,)),
            dma((count,)), dma((count,)),
            dma, dma, dma,
            dma, dma, dma,
            dma, dma, dma, pltpu.SemaphoreType.REGULAR,
        ],
        compiler_params=pltpu.CompilerParams(
            collective_id=0, has_side_effects=True, vmem_limit_bytes=48 * 1024 * 1024
        ),
    )(*(pltpu.with_memory_space_constraint(a, pltpu.HBM) for a in (
        grad_output, logits.T, chosen.T, slots.T, other_scores.T,
        hidden.reshape(window, capacity, hidden_units), down_weight.reshape(shard_rows, width),
    )))
    gradh, down, turned = (
        pltpu.with_memory_space_constraint(a, pltpu.VMEM) for a in (gradh, down, turned)
    )
    gradh, down, turned = pl.pallas_call(
        write_out,
        out_shape=tuple(jax.ShapeDtypeStruct(a.shape, a.dtype) for a in (gradh, down, turned)),
        in_specs=[vmem] * 3,
        out_specs=(hbm,) * 3,
        scratch_shapes=[dma((3,))],
        compiler_params=pltpu.CompilerParams(vmem_limit_bytes=8 * 1024 * 1024),
    )(gradh, down, turned)
    return (gradh.reshape(hidden.shape), down.reshape(1, shard_rows, width), turned.T)


def plain(grad_output, logits, chosen, slots, other_scores, hidden, down_weight):
    window = lax.axis_size("expert")
    capacity = hidden.shape[3]
    hidden_units = hidden.shape[4]
    model_width = grad_output.shape[1]
    shard_rows = down_weight.shape[1]
    raised = jnp.exp(logits)
    gating = raised / jnp.sum(raised, axis=1, keepdims=True)
    gate_sent = gating.astype(jnp.bfloat16)
    live_slot = slots < capacity
    target = jnp.where(live_slot, chosen * capacity + slots, window * capacity)
    columns = jnp.arange(window * capacity, dtype=jnp.int32)
    placing = (target[:, :, None] == columns[None, None, :]).astype(jnp.bfloat16)
    dispatch = jnp.sum(placing, axis=1)
    send_rows = jnp.einsum(
        "tr,td->rd", dispatch, grad_output, preferred_element_type=jnp.float32
    ).astype(jnp.bfloat16)
    send_gate = jnp.einsum(
        "tkr,tk->r", placing, gate_sent, preferred_element_type=jnp.float32
    ).astype(jnp.bfloat16)
    placing_float = placing.astype(jnp.float32)
    send_rows = send_rows.reshape(window, capacity, model_width)
    send_gate = send_gate.reshape(window, capacity)
    recv_rows, recv_gate = (
        lax.all_to_all(send_rows, "expert", split_axis=0, concat_axis=0, tiled=True),
        lax.all_to_all(send_gate, "expert", split_axis=0, concat_axis=0, tiled=True),
    )
    slot_rows = recv_rows.reshape(-1, model_width)
    slot_gate = recv_gate.reshape(-1).astype(jnp.float32)
    local_hidden = hidden.reshape(-1, hidden_units)
    scaled = (slot_gate[:, None] * slot_rows.astype(jnp.float32)).astype(jnp.bfloat16)
    weights = down_weight.reshape(shard_rows, model_width)
    product = lax.dot_general(
        slot_rows,
        lax.all_gather(weights, "dp", axis=0, tiled=True),
        (((1,), (1,)), ((), ())),
        preferred_element_type=jnp.float32,
    )
    grad_rows = lax.psum_scatter(
        lax.dot_general(
            local_hidden, scaled, (((0,), (0,)), ((), ())), preferred_element_type=jnp.float32
        ).astype(jnp.bfloat16),
        "dp",
        scatter_dimension=0,
        tiled=True,
    ).astype(jnp.float32)
    slot_scores = jnp.sum(local_hidden.astype(jnp.float32) * product, axis=1)
    grad_hidden = (slot_gate[:, None] * product).astype(jnp.bfloat16).reshape(hidden.shape)
    returned = lax.all_to_all(
        slot_scores.reshape(window, capacity), "expert", split_axis=0, concat_axis=0, tiled=True
    )
    token_scores = jnp.einsum(
        "tkr,r->tk", placing_float, returned.reshape(-1), precision=lax.Precision.HIGHEST
    )
    outside = jnp.where(chosen >= window, other_scores, jnp.float32(0.0))
    scores_all = jnp.where(live_slot, token_scores, outside)
    mean_score = jnp.sum(gating * scores_all, axis=1, keepdims=True)
    grad_logits = gating * (scores_all - mean_score)
    return (grad_hidden, grad_rows.reshape(1, shard_rows, model_width), grad_logits)


def body(grad_output, logits, chosen, slots, other_scores, hidden, down_weight):
    args = (grad_output, logits, chosen, slots, other_scores, hidden, down_weight)
    fits = (
        lax.axis_size("dp") % 2 == 0
        and lax.axis_size("dp") > 2
        and lax.axis_size("expert") == 4 * COLUMNS
        and hidden.shape[3] % 8 == 0
        and down_weight.shape[1] % 16 == 0
        and hidden.shape[4] % 128 == 0
        and grad_output.shape[0] == 128
        and grad_output.shape[1] % PIECE == 0
        and grad_output.shape[1] >= 2 * SMALL + 3 * PIECE
        and logits.shape[1] == 8
    )
    return fused(*args) if fits else plain(*args)


def solution(mesh):
    placed = (
        P(("expert", "dp"), None),
        P(("expert", "dp"), None),
        P(("expert", "dp"), None),
        P(("expert", "dp"), None),
        P(("expert", "dp"), None),
        P("expert", "dp", None, None, None),
        P("expert", "dp", None),
    )
    return jax.shard_map(
        body,
        mesh=mesh,
        in_specs=placed,
        out_specs=(
            P("expert", "dp", None, None, None),
            P("expert", "dp", None),
            P(("expert", "dp"), None),
        ),
        check_vma=False,
    )
```

time: 45.6 us -> 43.6 us (0.956)
  Pallas kernels: 44.8 us -> 42.7 us
    pallas_call x1, Pallas kernels: 43.4 us -> 41.4 us  [fused(): pl.pallas_call(functools.partial(kernel, window, shards, capacity, AHEAD,...]
where the time goes in v3:
time: 43.6 us; the launch traced here: 43.4 us
  Pallas kernels  42.7 us (98%)
  between operations  0.64 us (1%)
    pallas_call x1, Pallas kernels, fused(): pl.pallas_call(functools.partial(kernel, window, shards, capacity, AHEAD,...  41.4 us
    pallas_call x1, Pallas kernels, fused(): pl.pallas_call(write_out, out_shape=tuple((jax.ShapeDtypeStruct(a.shape,...  1.33 us

profile of v3, /device:TPU:0, one launch (start us, length us, event | category | flops | bytes accessed | tf_op | source)
XLA Modules:
  0.0 43.4 jit_solution(5097766545147934855)
XLA Ops:
  0.6 41.4 %shard_map.94 = (bf16[8,40,768]{2,1,0:T(8,128)(2,1)S(1)}, f32[192,2048]{1,0:T(8,128)S(1)}, f32[8,128]{1,0:T(8,128)S(1)}) custom-call(bf16[128,2048]{1,0:T(8,128)(2,1)} %token_hbm.1, f32[8,128]{1,0:T(8,128)} %bitcast.11, s32[8,128]{1,0:T(8,128)} %bitcast.12, s32[8,128]{1,0:T(8,128)} %bitcast.13, f32[8,128]{1,0:T(8,128)} %bitcast.14, ...), custom_call_target="tpu_custom_call" | custom-call | tf_op jit(solution)/shard_map/pallas_call | solution.py:561
  42.0 1.3 %shard_map.95 = (bf16[8,40,768]{2,1,0:T(8,128)(2,1)}, f32[192,2048]{1,0:T(8,128)}, f32[8,128]{1,0:T(8,128)}) custom-call(bf16[8,40,768]{2,1,0:T(8,128)(2,1)S(1)} %get-tuple-element.9.a, f32[192,2048]{1,0:T(8,128)S(1)} %get-tuple-element.10.b, f32[8,128]{1,0:T(8,128)S(1)} %get-tuple-element.11.c), custom_call_target="tpu_custom_call" | custom-call | tf_op jit(solution)/shard_map/pallas_call | solution.py:606

commit v4 on v3

--- a/solution.py
+++ b/solution.py
@@ -10,6 +10,8 @@
 MESH = pl.DeviceIdType.MESH
 PIECE = 256
 SMALL = 128
+HEADS = 1
+TAILS = 3
 AHEAD = 3
 NEAR_AHEAD = 7
 NEAR_LEAD = 3
@@ -19,15 +21,16 @@
 
 
 class Part:
-    def __init__(self, p, small, count, width):
+    def __init__(self, p, small, big):
         self.p = p
         self.small = small
+        past = p // (HEADS + big)
         if small:
-            self.index, self.size = p // (count - 1), SMALL
-            start = self.index * (width - SMALL)
+            self.index, self.size = p - big * past, SMALL
+            start = self.index * SMALL + past * (big * PIECE)
         else:
-            self.index, self.size = p - 1, PIECE
-            start = SMALL + self.index * PIECE
+            self.index, self.size = p - HEADS, PIECE
+            start = HEADS * SMALL + self.index * PIECE
         self.lanes = pl.ds(pl.multiple_of(start, 128), self.size)
 
     def of(self, pair):
@@ -54,24 +57,25 @@
     chips = shards // 2
     mate = (me, chip * 2 + 1 - core)
     tokens, width = token_ref.shape
-    count = rsend_b.shape[0] + 2
+    big = rsend_b.shape[0]
+    count = HEADS + big + TAILS
     rows = rsend_b.shape[2]
     slots_all = window * rows
     shard_rows, hidden_units = weight_ref.shape[0], hidden_ref.shape[2]
 
     def at(p, act):
         if isinstance(p, int):
-            act(Part(p, p in (0, count - 1), count, width))
+            act(Part(p, p < HEADS or p >= HEADS + big, big))
             return
-        small = (p == 0) | (p == count - 1)
+        small = (p < HEADS) | (p >= HEADS + big)
 
         @pl.when(small)
         def _():
-            act(Part(p, True, count, width))
+            act(Part(p, True, big))
 
         @pl.when(jnp.logical_not(small))
         def _():
-            act(Part(p, False, count, width))
+            act(Part(p, False, big))
 
     def flipped(mask):
         where = me
@@ -229,8 +233,9 @@
         return remote(part.of(csend), part.of(crecv), cs, cr.at[part.p], mate)
 
     def sum_copy(part, step):
+        mark = 1 + (part.p + 1) // count if part.small else 0
         return remote(
-            part.of(ysend).at[step - 1], part.of(yrecv).at[step - 1], cs, yr.at[part.p], across(step)
+            part.of(ysend).at[step - 1], part.of(yrecv).at[step - 1], cs, yr.at[mark], across(step)
         )
 
     at(0, fill)
@@ -394,6 +399,15 @@
     for p in range(pass_ahead):
         at(p, pass_weights)
 
+    def lift(part):
+        got = part.of(rrecv)[...].reshape(slots_all, part.size)
+        with jax.named_scope("w_mate"):
+            arrived(part.of(wfull).at[pl.ds(0, chips)], dr.at[part.p])
+        weights = part.of(wfull)[...].reshape(hidden_units, part.size)
+        upward[...] += lax.dot_general(
+            got, weights, (((1,), (1,)), ((), ())), preferred_element_type=jnp.float32
+        )
+
     def work(part):
         p = part.p
 
@@ -408,6 +422,10 @@
         @pl.when(inner == 0)
         def _():
             rows_in(window - 1)
+
+        @pl.when(p + 1 == count)
+        def _():
+            lift(part)
 
         got = part.of(rrecv)[...].reshape(slots_all, part.size)
         scaled = (gates[...].reshape(slots_all, 1) * got.astype(jnp.float32)).astype(jnp.bfloat16)
@@ -420,12 +438,9 @@
             part.of(own)[h] = jnp.dot(
                 hturn[2 * h + core], scaled, preferred_element_type=jnp.float32
             )
-        with jax.named_scope("w_mate"):
-            arrived(part.of(wfull).at[pl.ds(0, chips)], dr.at[p])
-        weights = part.of(wfull)[...].reshape(hidden_units, part.size)
-        upward[...] += lax.dot_general(
-            got, weights, (((1,), (1,)), ((), ())), preferred_element_type=jnp.float32
-        )
+        @pl.when(p + 1 < count)
+        def _():
+            lift(part)
 
     def finish(p, carry):
         @pl.when((inner == 1) & (p + relay_ahead < count))
@@ -463,8 +478,6 @@
         gradh_ref[s] = (gates[s, 0:capacity] * up).astype(jnp.bfloat16)
 
     def collect(part):
-        with jax.named_scope("w_sum"):
-            arrived(part.of(yrecv), yr.at[part.p])
         for step in range(1, chips):
             down_ref[:, part.lanes] += part.of(yrecv)[step - 1].astype(jnp.float32)
 
@@ -496,6 +509,9 @@
         at(p, collect)
         return carry
 
+    with jax.named_scope("w_sums"):
+        arrived(yrecv_b, yr.at[0])
+        arrived(yrecv_s.at[pl.ds(0, HEADS + TAILS - 1)], yr.at[1])
     lax.fori_loop(0, count - 1, collect_next, 0)
 
     with jax.named_scope("w_scores"):
@@ -508,6 +524,8 @@
     logit_ref[...] = gating * (scores_all - mean_score)
     settle(tsend, rs)
 
+    with jax.named_scope("w_sum"):
+        arrived(yrecv_s.at[HEADS + TAILS - 1], yr.at[2])
     at(count - 1, collect)
     for kind in range(2):
         arrived(ysend[kind], cs)
@@ -533,8 +551,9 @@
     shard_rows = down_weight.shape[1]
     rows = -(-capacity // 16) * 16
     chips = shards // 2
-    big = (width - 2 * SMALL) // PIECE
-    count = big + 2
+    ends = HEADS + TAILS
+    big = (width - ends * SMALL) // PIECE
+    count = big + ends
     vmem = pl.BlockSpec(memory_space=pltpu.VMEM)
     hbm = pl.BlockSpec(memory_space=pltpu.HBM)
     bf, f32, dma = jnp.bfloat16, jnp.float32, pltpu.SemaphoreType.DMA
@@ -586,8 +605,8 @@
             pltpu.VMEM((2, window // 2 * rows, tokens), bf),
             pltpu.VMEM((COLUMNS * rows, tokens), bf),
             *per_piece(big, PIECE),
-            *per_piece(2, SMALL),
-            dma((count,)), dma((count, chips - 1)), dma((count,)), dma((count,)), dma((count,)),
+            *per_piece(ends, SMALL),
+            dma((count,)), dma((count, chips - 1)), dma((count,)), dma((count,)), dma((3,)),
             dma((count,)), dma((count,)),
             dma, dma, dma,
             dma, dma, dma,
@@ -685,8 +704,8 @@
         and down_weight.shape[1] % 16 == 0
         and hidden.shape[4] % 128 == 0
         and grad_output.shape[0] == 128
-        and grad_output.shape[1] % PIECE == 0
-        and grad_output.shape[1] >= 2 * SMALL + 3 * PIECE
+        and (grad_output.shape[1] - (HEADS + TAILS) * SMALL) % PIECE == 0
+        and grad_output.shape[1] >= (HEADS + TAILS) * SMALL + 4 * PIECE
         and logits.shape[1] == 8
     )
     return fused(*args) if fits else plain(*args)

time: 43.6 us -> 43.4 us (level)
  no operation moved by 1% of the time
where the time goes in v4:
time: 43.4 us; the launch traced here: 43.2 us
  Pallas kernels  42.5 us (98%)
  between operations  0.64 us (1%)
    pallas_call x1, Pallas kernels, fused(): pl.pallas_call(functools.partial(kernel, window, shards, capacity, AHEAD,...  41.2 us
    pallas_call x1, Pallas kernels, fused(): pl.pallas_call(write_out, out_shape=tuple((jax.ShapeDtypeStruct(a.shape,...  1.33 us

profile of v4, /device:TPU:0, one launch (start us, length us, event | category | flops | bytes accessed | tf_op | source)
XLA Modules:
  0.0 43.2 jit_solution(14285331821141064665)
XLA Ops:
  0.6 41.2 %shard_map.94 = (bf16[8,40,768]{2,1,0:T(8,128)(2,1)S(1)}, f32[192,2048]{1,0:T(8,128)S(1)}, f32[8,128]{1,0:T(8,128)S(1)}) custom-call(bf16[128,2048]{1,0:T(8,128)(2,1)} %token_hbm.1, f32[8,128]{1,0:T(8,128)} %bitcast.11, s32[8,128]{1,0:T(8,128)} %bitcast.12, s32[8,128]{1,0:T(8,128)} %bitcast.13, f32[8,128]{1,0:T(8,128)} %bitcast.14, ...), custom_call_target="tpu_custom_call" | custom-call | tf_op jit(solution)/shard_map/pallas_call | solution.py:580
  41.9 1.3 %shard_map.95 = (bf16[8,40,768]{2,1,0:T(8,128)(2,1)}, f32[192,2048]{1,0:T(8,128)}, f32[8,128]{1,0:T(8,128)}) custom-call(bf16[8,40,768]{2,1,0:T(8,128)(2,1)S(1)} %get-tuple-element.9.a, f32[192,2048]{1,0:T(8,128)S(1)} %get-tuple-element.10.b, f32[8,128]{1,0:T(8,128)S(1)} %get-tuple-element.11.c), custom_call_target="tpu_custom_call" | custom-call | tf_op jit(solution)/shard_map/pallas_call | solution.py:625
